TPU v7x, 32 devices: a whole 2x2x4 slice. The times are simulated.
32 devices in a mesh: blk: 32 (over z, y, x, core).
Axes of the slice: x: 2, y: 2, z: 4, core: 2. Of those that a mesh axis runs over, the one named last changes fastest.
Arguments:
- geometry: float32 [8, 32768], P(None, 'blk'), may hold values from -1 to 9.333333, as said below
- currents: float32 [32, 32768], P(None, 'blk'), may hold values from -6 to 6
- net_ids: int32 [32768], P('blk'), may hold values from 0 to 3
- pair_on: int32 [32, 8], P('blk'), may hold values from 0 to 1, as said below
Outputs:
- voltage: float32 [32, 32768], P(None, 'blk')
Inputs may be any that keep to these rules, and one draw needn't show every extreme that they name: `geometry`: rows 0 to 1 lie in 0 to 32 / 6 + 4, row 2 in 0 to 0.2, rows 3 to 5 form a unit vector, row 6 lies in 0.2 to 2 and row 7 in 0.05 to 0.5. Symmetric: pair_on[b, 4 + d - 1] equals pair_on[(b + d) mod 32, d - 1] for d = 1 .. 4.
All inputs are finite; a program needn't handle non-finite values.
Results may differ from a plain program's by a relative error of at most 0.0003.
Values sent between devices are 32-bit elements; how exact they have to be, the bound alone decides.
A program may use at most 64 MiB of HBM per device.

v0:
```python
import functools

import jax
import jax.numpy as jnp
from jax import lax
from jax.experimental import pallas as pl
from jax.experimental.pallas import tpu as pltpu
from jax.sharding import PartitionSpec as P

MESH = pl.DeviceIdType.MESH
NETS = 4
GEO = 8
FEATURES = 128
GEO_AT = 112
CHUNK = 256
LANES = 256
F32 = jnp.float32
BF16 = jnp.bfloat16


def rounded(x):
    return x.astype(BF16).astype(F32)


def split(x):
    high = rounded(x)
    return high, rounded(x - high)


def split3(x):
    high = rounded(x)
    mid = rounded(x - high)
    return high, mid, rounded(x - high - mid)


def stack_rows(rows, wide):
    at = lax.broadcasted_iota(jnp.int32, (GEO, wide), 0)
    tiles = []
    for first in range(0, len(rows), GEO):
        tile = jnp.zeros((GEO, wide), F32)
        for k, row in enumerate(rows[first : first + GEO]):
            tile = jnp.where(at == k, row, tile)
        tiles.append(tile)
    return tiles


def other_features(geo, net):
    wide = geo.shape[1]
    scaled = geo * geo[6:7]
    highs, lows = [], []
    for n in range(NETS):
        high, low = split(scaled * jnp.where(net == n, F32(1.0), F32(0.5)))
        highs.append(high)
        lows.append(low)
    z, r = geo[2:3], geo[7:8]
    one = jnp.ones_like(z)
    ah, am, al = split3(z * z + r * r)
    zh, zm, zl = split3(z)
    near = stack_rows([ah, am, al, one, one, one, zh, zh, zh, zm, zm, zl], wide)
    pad = jnp.zeros((GEO, wide), F32)
    return jnp.concatenate(highs + lows + highs + near + [geo, pad], axis=0)


def own_features(geo, net):
    wide = geo.shape[1]
    at = lax.broadcasted_iota(jnp.int32, (GEO, wide), 0)
    scaled = jnp.where((at >= 3) & (at < 6), geo * (geo[6:7] * F32(0.1)), F32(0.0))
    highs, lows = [], []
    for n in range(NETS):
        high, low = split(jnp.where(net == n, scaled, F32(0.0)))
        highs.append(high)
        lows.append(low)
    z, r = geo[2:3], geo[7:8]
    one = jnp.ones_like(z)
    ah, am, al = split3(z * z + r * r)
    zh, zm, zl = (F32(-2.0) * part for part in split3(z))
    near = stack_rows([one, one, one, ah, am, al, zh, zm, zl, zh, zm, zh], wide)
    pad = jnp.zeros((GEO, wide), F32)
    product = jnp.concatenate(highs + highs + lows + [pad] * 4, axis=0)
    radial = jnp.concatenate([pad] * (3 * NETS) + near + [pad] * 2, axis=0)
    return product.astype(BF16), radial.astype(BF16)


def body(n, reach, geo, cur, net, pair, out, geo_in, cur_in, net_in, product, radial, send_sem, recv_sem):
    me = lax.axis_index("blk")
    seg = geo.shape[1]
    cols = cur.shape[0]
    offsets = [-(k + 1) for k in range(reach)] + [k + 1 for k in range(reach)]

    barrier = pltpu.get_barrier_semaphore()
    for o in offsets:
        pl.semaphore_signal(barrier, inc=1, device_id=(lax.rem(me + o + n, n),), device_id_type=MESH)
    pl.semaphore_wait(barrier, len(offsets))

    copies = {}
    order = [k for d in range(reach) for k in (d, reach + d)]
    for k in order:
        target = lax.rem(me - offsets[k] + n, n)
        for part, (src, dst) in enumerate(((geo, geo_in), (net, net_in), (cur, cur_in))):
            copy = pltpu.make_async_remote_copy(
                src_ref=src,
                dst_ref=dst.at[k],
                send_sem=send_sem.at[k, part],
                recv_sem=recv_sem.at[k, part],
                device_id=(target,),
                device_id_type=MESH,
            )
            copy.start()
            copies[k, part] = copy

    for first in range(0, seg, LANES):
        at = pl.ds(first, LANES)
        product[:, at], radial[:, at] = own_features(geo[:, at], net[:, at])
    out[...] = jnp.zeros_like(out)

    def tile(geo_o, cur_o, net_o, flag):
        @pl.loop(0, seg // CHUNK)
        def _(c):
            at = pl.ds(pl.multiple_of(c * CHUNK, CHUNK), CHUNK)
            feats = other_features(geo_o[:, at], net_o[:, at]).T
            low_feats = feats.astype(BF16)
            x_o = feats[:, GEO_AT : GEO_AT + 1]
            y_o = feats[:, GEO_AT + 1 : GEO_AT + 2]
            data = cur_o[:, at]
            if flag is not None:
                data = data * flag
            high = data.astype(BF16)
            both = jnp.concatenate([high, (data - high.astype(F32)).astype(BF16)], axis=0)
            for first in range(0, seg, LANES):
                own = pl.ds(first, LANES)
                g = jnp.dot(low_feats, product[:, own], preferred_element_type=F32)
                near = jnp.dot(low_feats, radial[:, own], preferred_element_type=F32)
                dx = geo[0:1, own] - x_o
                dy = geo[1:2, own] - y_o
                kern = g * lax.rsqrt(dx * dx + dy * dy + near)
                kh = kern.astype(BF16)
                kl = (kern - kh.astype(F32)).astype(BF16)
                v = jnp.dot(both, kh, preferred_element_type=F32) + jnp.dot(both, kl, preferred_element_type=F32)
                out[:, own] += v[:cols] + v[cols:]

    tile(geo, cur, net, None)

    per = lax.rem(me, 2 * reach)
    low_first = per >= reach

    @pl.loop(0, 2 * reach)
    def _(t):
        k = jnp.where(low_first, t, lax.rem(t + reach, 2 * reach))
        for part, (src, dst) in enumerate(((geo, geo_in), (net, net_in), (cur, cur_in))):
            pltpu.make_async_remote_copy(
                src_ref=src,
                dst_ref=dst.at[k],
                send_sem=send_sem.at[k, part],
                recv_sem=recv_sem.at[k, part],
                device_id=(lax.rem(me + 1, n),),
                device_id_type=MESH,
            ).wait_recv()
        flags = pair[...].astype(F32)
        lane = lax.broadcasted_iota(jnp.int32, flags.shape, 1)
        flag = jnp.sum(jnp.where(lane == k, flags, F32(0.0)), axis=1, keepdims=True)
        tile(geo_in.at[k], cur_in.at[k], net_in.at[k], flag)

    for copy in copies.values():
        copy.wait_send()


def shards(n, geometry, currents, net_ids, pair_on):
    reach = pair_on.shape[1] // 2
    seg = geometry.shape[1]
    cols = currents.shape[0]
    near = 2 * reach
    vmem = pl.BlockSpec(memory_space=pltpu.VMEM)
    return pl.pallas_call(
        functools.partial(body, n, reach),
        out_shape=jax.ShapeDtypeStruct((cols, seg), F32),
        in_specs=[vmem] * 4,
        out_specs=vmem,
        scratch_shapes=[
            pltpu.VMEM((near, GEO, seg), F32),
            pltpu.VMEM((near, cols, seg), F32),
            pltpu.VMEM((near, 1, seg), jnp.int32),
            pltpu.VMEM((FEATURES, seg), BF16),
            pltpu.VMEM((FEATURES, seg), BF16),
            pltpu.SemaphoreType.DMA((near, 3)),
            pltpu.SemaphoreType.DMA((near, 3)),
        ],
        compiler_params=pltpu.CompilerParams(collective_id=0, has_side_effects=True),
    )(geometry, currents, net_ids[None, :], pair_on)


def solution(mesh):
    return jax.shard_map(
        functools.partial(shards, mesh.shape["blk"]),
        mesh=mesh,
        in_specs=(P(None, "blk"), P(None, "blk"), P("blk"), P("blk", None)),
        out_specs=P(None, "blk"),
        check_vma=False,
    )
```

profile of v0, /device:TPU:0, one launch (start us, length us, event | category | flops | bytes accessed | tf_op | source)
XLA Modules:
  0.0 58.3 jit_solution(16409342996138645773)
XLA Ops:
  0.0 56.7 %shard_map.46 = f32[32,1024]{1,0:T(8,128)} custom-call(f32[8,1024]{1,0:T(8,128)} %geo.1, f32[32,1024]{1,0:T(8,128)} %cur.1, s32[1,1024]{1,0:T(1,128)} %bitcast.1, s32[1,8]{1,0:T(1,128)} %pair.1), custom_call_target="tpu_custom_call" | custom-call | tf_op jit(solution)/shard_map/pallas_call | solution.py:173
  56.7 1.6 %copy.6 = f32[32,1024]{1,0:T(8,128)} copy(f32[32,1024]{1,0:T(8,128)} %shard_map.46) | data formatting | bytes 262144
where the time goes:
time: 58.4 us; the launch traced here: 58.3 us
  Pallas kernels  56.7 us (97%)
  local copies, waits for them, and re-layouts  1.57 us (3%)
    pallas_call x1, Pallas kernels, shards(): pl.pallas_call(functools.partial(body, n, reach), out_shape=jax.ShapeDtyp...  56.7 us
    unnamed x1, local copies, waits for them, and re-layouts  1.57 us

commit v1 on v0

--- a/solution.py
+++ b/solution.py
@@ -13,7 +13,7 @@
 FEATURES = 128
 GEO_AT = 112
 CHUNK = 256
-LANES = 256
+LANES = 1024
 F32 = jnp.float32
 BF16 = jnp.bfloat16
 
@@ -121,6 +121,10 @@
             low_feats = feats.astype(BF16)
             x_o = feats[:, GEO_AT : GEO_AT + 1]
             y_o = feats[:, GEO_AT + 1 : GEO_AT + 2]
+            z_o = feats[:, GEO_AT + 2 : GEO_AT + 3]
+            r_o = feats[:, GEO_AT + 7 : GEO_AT + 8]
+            a_o = z_o * z_o + r_o * r_o
+            z_o = z_o + z_o
             data = cur_o[:, at]
             if flag is not None:
                 data = data * flag
@@ -129,7 +133,8 @@
             for first in range(0, seg, LANES):
                 own = pl.ds(first, LANES)
                 g = jnp.dot(low_feats, product[:, own], preferred_element_type=F32)
-                near = jnp.dot(low_feats, radial[:, own], preferred_element_type=F32)
+                a_i = geo[2:3, own] * geo[2:3, own] + geo[7:8, own] * geo[7:8, own]
+                near = (a_i + a_o) - geo[2:3, own] * z_o
                 dx = geo[0:1, own] - x_o
                 dy = geo[1:2, own] - y_o
                 kern = g * lax.rsqrt(dx * dx + dy * dy + near)

time: 58.4 us -> 51.2 us (0.88)
  Pallas kernels: 56.7 us -> 49.4 us
    pallas_call x1, Pallas kernels: 56.7 us -> 49.4 us  [shards(): pl.pallas_call(functools.partial(body, n, reach), out_shape=jax.ShapeDtyp...]
where the time goes in v1:
time: 51.2 us; the launch traced here: 51 us
  Pallas kernels  49.4 us (96%)
  local copies, waits for them, and re-layouts  1.57 us (3%)
    pallas_call x1, Pallas kernels, shards(): pl.pallas_call(functools.partial(body, n, reach), out_shape=jax.ShapeDtyp...  49.4 us
    unnamed x1, local copies, waits for them, and re-layouts  1.57 us

profile of v1, /device:TPU:0, one launch (start us, length us, event | category | flops | bytes accessed | tf_op | source)
XLA Modules:
  0.0 51.0 jit_solution(6148590947022950565)
XLA Ops:
  0.0 49.4 %shard_map.46 = f32[32,1024]{1,0:T(8,128)} custom-call(f32[8,1024]{1,0:T(8,128)} %geo.1, f32[32,1024]{1,0:T(8,128)} %cur.1, s32[1,1024]{1,0:T(1,128)} %bitcast.1, s32[1,8]{1,0:T(1,128)} %pair.1), custom_call_target="tpu_custom_call" | custom-call | tf_op jit(solution)/shard_map/pallas_call | solution.py:178
  49.5 1.6 %copy.6 = f32[32,1024]{1,0:T(8,128)} copy(f32[32,1024]{1,0:T(8,128)} %shard_map.46) | data formatting | bytes 262144
